TPU v7x, 32 devices: a whole 2x2x4 slice. The times are simulated.
32 devices in a mesh: dom: 16 (over z, y, x), grp: 2 (over core).
Axes of the slice: x: 2, y: 2, z: 4, core: 2. Of those that a mesh axis runs over, the one named last changes fastest.
Arguments:
- tangent_tiles: bfloat16 [4096, 128, 128], P(('grp', 'dom')), parts along dimension 0, may hold values from -0.5 to 0.5
- tile_blocks: int32 [2048, 2], P('dom'), may hold values from 0 to 127, as said below
- block_home: int32 [128], replicated, may hold values from 0 to 127, as said below
- tile_count: int32 [16], P('dom'), may hold values from 48 to 128, as said below
- basis: bfloat16 [16384, 256], P('dom'), may hold values from -0.29882812 to 0.29882812
Outputs:
- reduced: float32 [512, 256], P('grp'), parts along dimension 0
There are 2 independent parts, one for each index of `grp`. A program takes and returns all parts, laid end to end along the dimension named above; an argument that names none is the same for every part. Nothing has to cross between parts.
Inputs may be any that keep to these rules, and one draw needn't show every extreme that they name: `tile_blocks`: every row block named by a device's tile slots has its position held by one of the devices with dom index from that device's index - 4 to its index + 8 // 2 - 1, taken cyclically. Among the row blocks named by one device's 128 slots, at most 2 distinct ones have their position held by any one device; every device reaches 2 for some holder. `block_home`: A permutation of the row blocks. `tile_count`: some device has exactly 128 live slots.
All inputs are finite; a program needn't handle non-finite values.
Results may differ from a plain program's by a relative error of at most 0.0029.
Values may be sent and summed in bfloat16 or wider, within the bound.
A program may use at most 64 MiB of HBM per device.

v0:
```python
import jax
import jax.numpy as jnp
from jax import lax
from jax.sharding import PartitionSpec as P

CAP = 2
NEAR = 8
GROUP = 16


def shifted(value, axis, steps):
    count = lax.axis_size(axis)
    pairs = [(source, (source + steps) % count) for source in range(count)]
    return lax.ppermute(value, axis, pairs)


def on_device(tangent_tiles, tile_blocks, block_home, tile_count, basis):
    ndom = lax.axis_size("dom")
    tile_dev = tangent_tiles.shape[0]
    block = tangent_tiles.shape[1]
    rank = basis.shape[1]
    blk_dev = basis.shape[0] // block
    stored = basis.reshape(blk_dev, block, rank)
    place = jnp.take(block_home, tile_blocks.reshape(-1), axis=0)
    places = jnp.arange(ndom * blk_dev, dtype=jnp.int32)
    wanted = jnp.any(place[:, None] == places[None, :], axis=0).astype(jnp.int32)
    wanted = wanted.reshape(ndom, blk_dev)
    order = jnp.cumsum(wanted, axis=1) - 1
    levels = jnp.arange(CAP, dtype=jnp.int32)
    chosen = (wanted[:, :, None] == 1) & (order[:, :, None] == levels[None, None, :])
    local_ids = jnp.arange(blk_dev, dtype=jnp.int32)[None, :, None]
    requests = jnp.sum(jnp.where(chosen, local_ids, 0), axis=1)
    holder = place // blk_dev
    flat_order = order.reshape(-1)
    level_of = jnp.take(flat_order, place, axis=0)
    myself = lax.axis_index("dom")
    pieces = []
    for step_k in range(NEAR):
        away = step_k - NEAR // 2
        target = (myself + away) % ndom
        asking = lax.dynamic_index_in_dim(requests, target, 0, keepdims=False)
        if away == 0:
            pieces.append(jnp.take(stored, asking, axis=0))
        else:
            asked = shifted(asking, "dom", away)
            served = jnp.take(stored, asked, axis=0)
            pieces.append(shifted(served, "dom", -away))
    fetched = jnp.concatenate(pieces, axis=0)
    window_pos = (holder - myself + NEAR // 2) % ndom
    slot_of = window_pos * CAP + level_of
    slot_of = slot_of.reshape(tile_dev, 2)
    live = (jnp.arange(tile_dev, dtype=jnp.int32) < tile_count[0]).astype(jnp.float32)

    def project(step, total):
        begin = step * GROUP
        tile_set = lax.dynamic_slice_in_dim(tangent_tiles, begin, GROUP, 0)
        link_set = lax.dynamic_slice_in_dim(slot_of, begin, GROUP, 0)
        live_set = lax.dynamic_slice_in_dim(live, begin, GROUP, 0)
        cols = jnp.take(fetched, link_set[:, 1], axis=0)
        rows = jnp.take(fetched, link_set[:, 0], axis=0)
        right = jnp.einsum("tab,tbr->tar", tile_set, cols, preferred_element_type=jnp.float32)
        right = (right * live_set[:, None, None]).astype(jnp.bfloat16)
        return total + jnp.einsum(
            "ar,as->rs",
            rows.reshape(GROUP * block, rank),
            right.reshape(GROUP * block, rank),
            preferred_element_type=jnp.float32,
        )

    partial_sum = lax.fori_loop(0, tile_dev // GROUP, project, jnp.zeros((rank, rank), jnp.float32))
    reduced = lax.psum(partial_sum, "dom")
    return reduced


def solution(mesh):
    return jax.shard_map(
        on_device,
        mesh=mesh,
        in_specs=(P(("grp", "dom"), None, None), P("dom", None), P(), P("dom"), P("dom", None)),
        out_specs=P("grp", None),
        check_vma=False,
    )
```

profile of v0, /device:TPU:0, one launch (start us, length us, event | category | flops | bytes accessed | tf_op | source)
XLA Modules:
  0.0 211.4 jit_solution(7998382532682025767)
XLA Ops:
  7.5 1.9 gather_fusion.2
  10.3 4.0 %collective-permute-start.12 = (s32[2]{0:T(128)S(1)}, s32[2]{0:T(128)S(1)}, u32[]{:S(2)}, u32[]{:S(2)}) collective-permute-start(s32[2]{0:T(128)S(1)} %get-tuple-element.157), channel_id=1, source_target_pairs={{0,6},{2,8},{4,10},{6,12},{8,14},{10,16},{12,18},{14,20},{16,22},{... | collective-permute-start | bytes 32 | tf_op jit(solution)/shard_map/ppermute | solution.py:14
  14.3 1.5 collective-permute-start.10
  16.4 5.0 %collective-permute-start.6 = (s32[2]{0:T(128)S(1)}, s32[2]{0:T(128)S(1)}, u32[]{:S(2)}, u32[]{:S(2)}) collective-permute-start(s32[2]{0:T(128)S(1)} %get-tuple-element.161), channel_id=1, source_target_pairs={{0,30},{2,0},{4,2},{6,4},{8,6},{10,8},{12,10},{14,12},{16,14},{18,... | collective-permute-start | bytes 32 | tf_op jit(solution)/shard_map/ppermute | solution.py:14
  22.8 1.9 gather_fusion.3
  25.9 1.5 collective-permute-start
  27.5 2.5 %collective-permute-done.2 = s32[2]{0:T(128)S(1)} collective-permute-done((s32[2]{0:T(128)S(1)}, s32[2]{0:T(128)S(1)}, u32[]{:S(2)}, u32[]{:S(2)}) %collective-permute-start.2) | collective-permute-done | bytes 40 | tf_op jit(solution)/shard_map/ppermute | solution.py:14
  34.1 5.0 %collective-permute-start.13 = (bf16[2,128,256]{2,1,0:T(8,128)(2,1)S(1)}, bf16[2,128,256]{2,1,0:T(8,128)(2,1)S(1)}, u32[]{:S(2)}, u32[]{:S(2)}) collective-permute-start(bf16[2,128,256]{2,1,0:T(8,128)(2,1)S(1)} %broadcast_select_fusion), channel_id=1, source_target_pairs={{0,26},{2,28},{4,30},{6,0},{8,2},{10,4},{12,6},{14,8},{16,10},{18,... | collective-permute-start | bytes 393224 | tf_op jit(solution)/shard_map/ppermute | solution.py:14
  39.4 1.5 collective-permute-start.9
  41.0 2.0 collective-permute-start.3
  43.4 6.5 %collective-permute-done.1 = bf16[2,128,256]{2,1,0:T(8,128)(2,1)S(1)} collective-permute-done((bf16[2,128,256]{2,1,0:T(8,128)(2,1)S(1)}, bf16[2,128,256]{2,1,0:T(8,128)(2,1)S(1)}, u32[]{:S(2)}, u32[]{:S(2)}) %collective-permute-start.1) | collective-permute-done | bytes 131104 | tf_op jit(solution)/shard_map/ppermute | solution.py:14
  51.6 6.0 %collective-permute-done.5 = bf16[2,128,256]{2,1,0:T(8,128)(2,1)S(1)} collective-permute-done((bf16[2,128,256]{2,1,0:T(8,128)(2,1)S(1)}, bf16[2,128,256]{2,1,0:T(8,128)(2,1)S(1)}, u32[]{:S(2)}, u32[]{:S(2)}) %collective-permute-start.5) | collective-permute-done | bytes 131104 | tf_op jit(solution)/shard_map/ppermute | solution.py:14
  57.6 2.5 %collective-permute-done.7 = bf16[2,128,256]{2,1,0:T(8,128)(2,1)S(1)} collective-permute-done((bf16[2,128,256]{2,1,0:T(8,128)(2,1)S(1)}, bf16[2,128,256]{2,1,0:T(8,128)(2,1)S(1)}, u32[]{:S(2)}, u32[]{:S(2)}) %collective-permute-start.7) | collective-permute-done | bytes 131104 | tf_op jit(solution)/shard_map/ppermute | solution.py:14
  60.3 37.5 %while.14 = (s32[]{:T(128)}, f32[256,256]{1,0:T(8,128)S(1)}, s32[128,2]{0,1:T(2,128)S(1)}, bf16[16,128,256]{2,1,0:T(8,128)(2,1)S(1)}, bf16[128,128,128]{2,1,0:T(...) while((s32[]{:T(128)}, f32[256,256]{1,0:T(8,128)S(1)}, ...), condition=%wide.region_4.8_spmd.clone, body=%wide.region_3.7_spmd.clone.sunk | while | flops 404883648 | bytes 7349425 | solution.py:70
  61.1 1.6 gather_fusion.1
  62.7 2.3 %fusion.38 = f32[256,256]{1,0:T(8,128)S(1)} fusion(bf16[16,128,256]{2,1,0:T(8,128)(2,1)S(1)} %gather_fusion, bf16[16,128,256]{2,1,0:T(8,128)(2,1)} %gather_fusion.1, f32[16]{0:T(128)S(1)} %dynamic_slice.90, pred[16]{0:T(512)(128)(4,1)S(1)} %get-tuple-element.246, pred[16]{0:T(512)(128)(4,1)S(1)} %get-tuple-element.247, ...), kind=kOutput, calls=%fused_computation.15.clone.1 | convolution fusion | flops 404881408 | bytes 3145829 | tf_op jit(solution)/shard_map/while/body/eval_jaxpr/ar,as->rs/dot_general | solution.py:63
  65.8 1.6 gather_fusion.1
  67.4 2.3 %fusion.38 = f32[256,256]{1,0:T(8,128)S(1)} fusion(bf16[16,128,256]{2,1,0:T(8,128)(2,1)S(1)} %gather_fusion, bf16[16,128,256]{2,1,0:T(8,128)(2,1)} %gather_fusion.1, f32[16]{0:T(128)S(1)} %dynamic_slice.90, pred[16]{0:T(512)(128)(4,1)S(1)} %get-tuple-element.246, pred[16]{0:T(512)(128)(4,1)S(1)} %get-tuple-element.247, ...), kind=kOutput, calls=%fused_computation.15.clone.1 | convolution fusion | flops 404881408 | bytes 3145829 | tf_op jit(solution)/shard_map/while/body/eval_jaxpr/ar,as->rs/dot_general | solution.py:63
  70.5 1.6 gather_fusion.1
  72.1 2.3 %fusion.38 = f32[256,256]{1,0:T(8,128)S(1)} fusion(bf16[16,128,256]{2,1,0:T(8,128)(2,1)S(1)} %gather_fusion, bf16[16,128,256]{2,1,0:T(8,128)(2,1)} %gather_fusion.1, f32[16]{0:T(128)S(1)} %dynamic_slice.90, pred[16]{0:T(512)(128)(4,1)S(1)} %get-tuple-element.246, pred[16]{0:T(512)(128)(4,1)S(1)} %get-tuple-element.247, ...), kind=kOutput, calls=%fused_computation.15.clone.1 | convolution fusion | flops 404881408 | bytes 3145829 | tf_op jit(solution)/shard_map/while/body/eval_jaxpr/ar,as->rs/dot_general | solution.py:63
  75.2 1.6 gather_fusion.1
  76.8 2.3 %fusion.38 = f32[256,256]{1,0:T(8,128)S(1)} fusion(bf16[16,128,256]{2,1,0:T(8,128)(2,1)S(1)} %gather_fusion, bf16[16,128,256]{2,1,0:T(8,128)(2,1)} %gather_fusion.1, f32[16]{0:T(128)S(1)} %dynamic_slice.90, pred[16]{0:T(512)(128)(4,1)S(1)} %get-tuple-element.246, pred[16]{0:T(512)(128)(4,1)S(1)} %get-tuple-element.247, ...), kind=kOutput, calls=%fused_computation.15.clone.1 | convolution fusion | flops 404881408 | bytes 3145829 | tf_op jit(solution)/shard_map/while/body/eval_jaxpr/ar,as->rs/dot_general | solution.py:63
  79.9 1.6 gather_fusion.1
  81.5 2.3 %fusion.38 = f32[256,256]{1,0:T(8,128)S(1)} fusion(bf16[16,128,256]{2,1,0:T(8,128)(2,1)S(1)} %gather_fusion, bf16[16,128,256]{2,1,0:T(8,128)(2,1)} %gather_fusion.1, f32[16]{0:T(128)S(1)} %dynamic_slice.90, pred[16]{0:T(512)(128)(4,1)S(1)} %get-tuple-element.246, pred[16]{0:T(512)(128)(4,1)S(1)} %get-tuple-element.247, ...), kind=kOutput, calls=%fused_computation.15.clone.1 | convolution fusion | flops 404881408 | bytes 3145829 | tf_op jit(solution)/shard_map/while/body/eval_jaxpr/ar,as->rs/dot_general | solution.py:63
  84.5 1.6 gather_fusion.1
  86.2 2.3 %fusion.38 = f32[256,256]{1,0:T(8,128)S(1)} fusion(bf16[16,128,256]{2,1,0:T(8,128)(2,1)S(1)} %gather_fusion, bf16[16,128,256]{2,1,0:T(8,128)(2,1)} %gather_fusion.1, f32[16]{0:T(128)S(1)} %dynamic_slice.90, pred[16]{0:T(512)(128)(4,1)S(1)} %get-tuple-element.246, pred[16]{0:T(512)(128)(4,1)S(1)} %get-tuple-element.247, ...), kind=kOutput, calls=%fused_computation.15.clone.1 | convolution fusion | flops 404881408 | bytes 3145829 | tf_op jit(solution)/shard_map/while/body/eval_jaxpr/ar,as->rs/dot_general | solution.py:63
  89.2 1.6 gather_fusion.1
  90.8 2.3 %fusion.38 = f32[256,256]{1,0:T(8,128)S(1)} fusion(bf16[16,128,256]{2,1,0:T(8,128)(2,1)S(1)} %gather_fusion, bf16[16,128,256]{2,1,0:T(8,128)(2,1)} %gather_fusion.1, f32[16]{0:T(128)S(1)} %dynamic_slice.90, pred[16]{0:T(512)(128)(4,1)S(1)} %get-tuple-element.246, pred[16]{0:T(512)(128)(4,1)S(1)} %get-tuple-element.247, ...), kind=kOutput, calls=%fused_computation.15.clone.1 | convolution fusion | flops 404881408 | bytes 3145829 | tf_op jit(solution)/shard_map/while/body/eval_jaxpr/ar,as->rs/dot_general | solution.py:63
  93.9 1.6 gather_fusion.1
  95.5 2.3 %fusion.38 = f32[256,256]{1,0:T(8,128)S(1)} fusion(bf16[16,128,256]{2,1,0:T(8,128)(2,1)S(1)} %gather_fusion, bf16[16,128,256]{2,1,0:T(8,128)(2,1)} %gather_fusion.1, f32[16]{0:T(128)S(1)} %dynamic_slice.90, pred[16]{0:T(512)(128)(4,1)S(1)} %get-tuple-element.246, pred[16]{0:T(512)(128)(4,1)S(1)} %get-tuple-element.247, ...), kind=kOutput, calls=%fused_computation.15.clone.1 | convolution fusion | flops 404881408 | bytes 3145829 | tf_op jit(solution)/shard_map/while/body/eval_jaxpr/ar,as->rs/dot_general | solution.py:63
  98.5 104.3 %all-reduce.2.cloned.1.call-done = f32[256,256]{1,0:T(8,128)} async-done(((f32[256,256]{1,0:T(8,128)}), f32[256,256]{1,0:T(8,128)}) %all-reduce.2.cloned.1.call-update) | async-done | bytes 262160 | tf_op jit(solution)/shard_map/psum | solution.py:71
  202.9 1.7 copy.36
  (126 shorter events, 17.7 us)
Async XLA Ops:
  6.5 18.3 %copy-start = (bf16[1024,256]{1,0:T(8,128)(2,1)S(1)}, bf16[1024,256]{1,0:T(8,128)(2,1)}, u32[]{:S(2)}) copy-start(bf16[1024,256]{1,0:T(8,128)(2,1)} %param.17) | copy-start | bytes 1572868
  6.5 196.3 %all-reduce.2.cloned.1.call-start = ((), (), s32[]{:S(2)}) async-start(), calls=%async_computation | async-start | bytes 524288 | tf_op jit(solution)/shard_map/psum | solution.py:71
  10.3 15.1 %collective-permute-start.12 = (s32[2]{0:T(128)S(1)}, s32[2]{0:T(128)S(1)}, u32[]{:S(2)}, u32[]{:S(2)}) collective-permute-start(s32[2]{0:T(128)S(1)} %get-tuple-element.157), channel_id=1, source_target_pairs={{0,6},{2,8},{4,10},{6,12},{8,14},{10,16},{12,18},{14,20},{16,22},{... | collective-permute-start | bytes 32 | tf_op jit(solution)/shard_map/ppermute | solution.py:14
  14.3 11.6 %collective-permute-start.10 = (s32[2]{0:T(128)S(1)}, s32[2]{0:T(128)S(1)}, u32[]{:S(2)}, u32[]{:S(2)}) collective-permute-start(s32[2]{0:T(128)S(1)} %get-tuple-element.158), channel_id=1, source_target_pairs={{0,4},{2,6},{4,8},{6,10},{8,12},{10,14},{12,16},{14,18},{16,20},{1... | collective-permute-start | bytes 32 | tf_op jit(solution)/shard_map/ppermute | solution.py:14
  15.8 11.6 %collective-permute-start.8 = (s32[2]{0:T(128)S(1)}, s32[2]{0:T(128)S(1)}, u32[]{:S(2)}, u32[]{:S(2)}) collective-permute-start(s32[2]{0:T(128)S(1)} %get-tuple-element.159), channel_id=1, source_target_pairs={{0,2},{2,4},{4,6},{6,8},{8,10},{10,12},{12,14},{14,16},{16,18},{18... | collective-permute-start | bytes 32 | tf_op jit(solution)/shard_map/ppermute | solution.py:14
  16.4 11.0 %collective-permute-start.6 = (s32[2]{0:T(128)S(1)}, s32[2]{0:T(128)S(1)}, u32[]{:S(2)}, u32[]{:S(2)}) collective-permute-start(s32[2]{0:T(128)S(1)} %get-tuple-element.161), channel_id=1, source_target_pairs={{0,30},{2,0},{4,2},{6,4},{8,6},{10,8},{12,10},{14,12},{16,14},{18,... | collective-permute-start | bytes 32 | tf_op jit(solution)/shard_map/ppermute | solution.py:14
  21.5 6.0 %collective-permute-start.4 = (s32[2]{0:T(128)S(1)}, s32[2]{0:T(128)S(1)}, u32[]{:S(2)}, u32[]{:S(2)}) collective-permute-start(s32[2]{0:T(128)S(1)} %get-tuple-element.162), channel_id=1, source_target_pairs={{0,28},{2,30},{4,0},{6,2},{8,4},{10,6},{12,8},{14,10},{16,12},{18,... | collective-permute-start | bytes 32 | tf_op jit(solution)/shard_map/ppermute | solution.py:14
  25.5 4.5 %collective-permute-start.2 = (s32[2]{0:T(128)S(1)}, s32[2]{0:T(128)S(1)}, u32[]{:S(2)}, u32[]{:S(2)}) collective-permute-start(s32[2]{0:T(128)S(1)} %get-tuple-element.163), channel_id=1, source_target_pairs={{0,26},{2,28},{4,30},{6,0},{8,2},{10,4},{12,6},{14,8},{16,10},{18,... | collective-permute-start | bytes 32 | tf_op jit(solution)/shard_map/ppermute | solution.py:14
  25.9 4.2 %collective-permute-start = (s32[2]{0:T(128)S(1)}, s32[2]{0:T(128)S(1)}, u32[]{:S(2)}, u32[]{:S(2)}) collective-permute-start(s32[2]{0:T(128)S(1)} %get-tuple-element.164), channel_id=1, source_target_pairs={{0,24},{2,26},{4,28},{6,30},{8,0},{10,2},{12,4},{14,6},{16,8},{18,... | collective-permute-start | bytes 32 | tf_op jit(solution)/shard_map/ppermute | solution.py:14
  34.1 26.2 %collective-permute-start.13 = (bf16[2,128,256]{2,1,0:T(8,128)(2,1)S(1)}, bf16[2,128,256]{2,1,0:T(8,128)(2,1)S(1)}, u32[]{:S(2)}, u32[]{:S(2)}) collective-permute-start(bf16[2,128,256]{2,1,0:T(8,128)(2,1)S(1)} %broadcast_select_fusion), channel_id=1, source_target_pairs={{0,26},{2,28},{4,30},{6,0},{8,2},{10,4},{12,6},{14,8},{16,10},{18,... | collective-permute-start | bytes 393224 | tf_op jit(solution)/shard_map/ppermute | solution.py:14
  39.2 21.1 %collective-permute-start.11 = (bf16[2,128,256]{2,1,0:T(8,128)(2,1)S(1)}, bf16[2,128,256]{2,1,0:T(8,128)(2,1)S(1)}, u32[]{:S(2)}, u32[]{:S(2)}) collective-permute-start(bf16[2,128,256]{2,1,0:T(8,128)(2,1)S(1)} %broadcast_select_fusion.1), channel_id=1, source_target_pairs={{0,28},{2,30},{4,0},{6,2},{8,4},{10,6},{12,8},{14,10},{16,12},{18,... | collective-permute-start | bytes 393224 | tf_op jit(solution)/shard_map/ppermute | solution.py:14
  39.4 20.9 %collective-permute-start.9 = (bf16[2,128,256]{2,1,0:T(8,128)(2,1)S(1)}, bf16[2,128,256]{2,1,0:T(8,128)(2,1)S(1)}, u32[]{:S(2)}, u32[]{:S(2)}) collective-permute-start(bf16[2,128,256]{2,1,0:T(8,128)(2,1)S(1)} %broadcast_select_fusion.2), channel_id=1, source_target_pairs={{0,30},{2,0},{4,2},{6,4},{8,6},{10,8},{12,10},{14,12},{16,14},{18,... | collective-permute-start | bytes 393224 | tf_op jit(solution)/shard_map/ppermute | solution.py:14
  41.0 10.5 %collective-permute-start.3 = (bf16[2,128,256]{2,1,0:T(8,128)(2,1)S(1)}, bf16[2,128,256]{2,1,0:T(8,128)(2,1)S(1)}, u32[]{:S(2)}, u32[]{:S(2)}) collective-permute-start(bf16[2,128,256]{2,1,0:T(8,128)(2,1)S(1)} %broadcast_select_fusion.5), channel_id=1, source_target_pairs={{0,6},{2,8},{4,10},{6,12},{8,14},{10,16},{12,18},{14,20},{16,22},{... | collective-permute-start | bytes 393224 | tf_op jit(solution)/shard_map/ppermute | solution.py:14
  43.1 6.8 %collective-permute-start.1 = (bf16[2,128,256]{2,1,0:T(8,128)(2,1)S(1)}, bf16[2,128,256]{2,1,0:T(8,128)(2,1)S(1)}, u32[]{:S(2)}, u32[]{:S(2)}) collective-permute-start(bf16[2,128,256]{2,1,0:T(8,128)(2,1)S(1)} %broadcast_select_fusion.6), channel_id=1, source_target_pairs={{0,8},{2,10},{4,12},{6,14},{8,16},{10,18},{12,20},{14,22},{16,24},... | collective-permute-start | bytes 393224 | tf_op jit(solution)/shard_map/ppermute | solution.py:14
  49.9 7.7 %collective-permute-start.5 = (bf16[2,128,256]{2,1,0:T(8,128)(2,1)S(1)}, bf16[2,128,256]{2,1,0:T(8,128)(2,1)S(1)}, u32[]{:S(2)}, u32[]{:S(2)}) collective-permute-start(bf16[2,128,256]{2,1,0:T(8,128)(2,1)S(1)} %broadcast_select_fusion.4), channel_id=1, source_target_pairs={{0,4},{2,6},{4,8},{6,10},{8,12},{10,14},{12,16},{14,18},{16,20},{1... | collective-permute-start | bytes 393224 | tf_op jit(solution)/shard_map/ppermute | solution.py:14
  51.5 8.6 %collective-permute-start.7 = (bf16[2,128,256]{2,1,0:T(8,128)(2,1)S(1)}, bf16[2,128,256]{2,1,0:T(8,128)(2,1)S(1)}, u32[]{:S(2)}, u32[]{:S(2)}) collective-permute-start(bf16[2,128,256]{2,1,0:T(8,128)(2,1)S(1)} %broadcast_select_fusion.3), channel_id=1, source_target_pairs={{0,2},{2,4},{4,6},{6,8},{8,10},{10,12},{12,14},{14,16},{16,18},{18... | collective-permute-start | bytes 393224 | tf_op jit(solution)/shard_map/ppermute | solution.py:14
  97.8 0.7 copy-start.1
Sparse Core Ops, SparseCore 0:
  98.6 104.1 all-reduce.1
where the time goes:
time: 212 us; the launch traced here: 211 us
  waiting for transfers between devices  122 us (58%)
  local copies, waits for them, and re-layouts  31.4 us (15%)
  starting transfers between devices  23.9 us (11%)
  matrix products  18 us (8%)
  between operations  14.5 us (7%)
    psum x1, waiting for transfers between devices, on_device(): reduced = lax.psum(partial_sum, 'dom')  104 us
    ppermute x14, starting transfers between devices, shifted(): return lax.ppermute(value, axis, pairs)  23.9 us
    dot_general x8, matrix products, project(): jnp.einsum('ar,as->rs', rows.reshape(GROUP * block, rank), right.reshape(...  18 us
    ppermute x14, waiting for transfers between devices, shifted(): return lax.ppermute(value, axis, pairs)  17.6 us
    gather x8, local copies, waits for them, and re-layouts, project(): rows = jnp.take(fetched, link_set[:, 0], axis=0)  12.8 us
    gather x8, local copies, waits for them, and re-layouts, project(): cols = jnp.take(fetched, link_set[:, 1], axis=0)  4.91 us
  transfers between devices with their start and end apart: 15, of which 5 were waited for; matrix products, arithmetic and copies ran while one was open for 2% of the time, Pallas kernels for 0%

commit v1 on v0

v1 whole, which is shorter than its diff:
```python
import functools

import jax
import jax.numpy as jnp
from jax import lax
from jax.experimental import pallas as pl
from jax.experimental.pallas import tpu as pltpu
from jax.sharding import PartitionSpec as P

CAP = 2
NEAR = 8
GROUP = 16
LOADS = 4
MESH = pl.DeviceIdType.MESH


def dot(a, b):
    return jnp.dot(a, b, preferred_element_type=jnp.float32)


def within(index, size):
    return jnp.minimum(jnp.maximum(index, 0), size - 1)


def kernel(ndom, ngrp, tb_ref, home_ref, count_ref, basis_ref, tiles_hbm, out_ref,
           tiles, req_out, req_in, req_s, slot_v, slot_s, served, fetched, turned,
           part, rs_in, ag, acc, tile_sem, req_send, req_recv, table_sem, slot_sem,
           blk_send, blk_recv, fwd_send, fwd_recv, rs_send, rs_recv, ag_send, ag_recv):
    me = lax.axis_index("dom")
    grp = lax.axis_index("grp")
    paired = ngrp == CAP
    ntile = tiles.shape[0]
    nblk = home_ref.shape[1]
    blk_dev = nblk // ndom
    half = NEAR // 2
    here = NEAR // 2

    barrier = pltpu.get_barrier_semaphore()
    for s in range(1, ndom):
        peer = lax.rem(me + s, ndom)
        pl.semaphore_signal(barrier, inc=1, device_id={"dom": peer, "grp": grp}, device_id_type=MESH)
    if paired:
        pl.semaphore_signal(barrier, inc=1, device_id={"dom": me, "grp": 1 - grp}, device_id_type=MESH)

    per = ntile // LOADS
    loads = [
        pltpu.make_async_copy(tiles_hbm.at[pl.ds(i * per, per)], tiles.at[pl.ds(i * per, per)], tile_sem.at[i])
        for i in range(LOADS)
    ]
    for load in loads:
        load.start()

    pos = lax.broadcasted_iota(jnp.int32, (nblk, nblk), 0)
    other = lax.broadcasted_iota(jnp.int32, (nblk, nblk), 1)
    moved = jnp.where(pos == home_ref[...], 1.0, 0.0).astype(jnp.bfloat16)
    ids = lax.broadcasted_iota(jnp.int32, (nblk, ntile), 0)
    at_row = dot(moved, jnp.where(ids == tb_ref[0:1, :], 1.0, 0.0).astype(jnp.bfloat16))
    at_col = dot(moved, jnp.where(ids == tb_ref[1:2, :], 1.0, 0.0).astype(jnp.bfloat16))
    wanted = jnp.max(jnp.maximum(at_row, at_col), axis=1, keepdims=True)
    wanted = jnp.broadcast_to(wanted, (nblk, 128))
    before = jnp.where((pos // blk_dev == other // blk_dev) & (other < pos), 1.0, 0.0).astype(jnp.bfloat16)
    order = dot(before, wanted.astype(jnp.bfloat16))
    lane_pos = lax.broadcasted_iota(jnp.int32, (nblk, 128), 0)
    local = lax.rem(lane_pos, blk_dev).astype(jnp.float32)
    near = lax.broadcasted_iota(jnp.int32, (NEAR, nblk), 0)
    near_pos = lax.broadcasted_iota(jnp.int32, (NEAR, nblk), 1)
    holder = lax.rem(near + (me + ndom - half), ndom)
    group = jnp.where(near_pos // blk_dev == holder, 1.0, 0.0).astype(jnp.bfloat16)
    for level in range(CAP):
        chosen = jnp.where(order == float(level), wanted * local, 0.0)
        table = dot(group, chosen.astype(jnp.bfloat16)).astype(jnp.int32)
        for k in range(NEAR):
            req_out[k, level:level + 1, :] = table[k:k + 1, :]
    window = lax.rem(lane_pos // blk_dev + (2 * ndom + half) - me, ndom)
    window = jnp.minimum(window, NEAR - 1)
    slot_map = (window * CAP).astype(jnp.float32) + order
    slot_map = jnp.broadcast_to(slot_map[:, 0:1], (nblk, ntile))
    slot_v[0:1, :] = jnp.sum(at_row * slot_map, axis=0, keepdims=True).astype(jnp.int32)
    slot_v[1:2, :] = jnp.sum(at_col * slot_map, axis=0, keepdims=True).astype(jnp.int32)

    pl.semaphore_wait(barrier, ndom - 1 + (1 if paired else 0))

    steps = [k for k in range(NEAR) if k != here]
    asks = {}
    for k in steps:
        target = lax.rem(me + (k - half + ndom), ndom)
        asks[k] = pltpu.make_async_remote_copy(
            src_ref=req_out.at[k], dst_ref=req_in.at[k], send_sem=req_send.at[k], recv_sem=req_recv.at[k],
            device_id={"dom": target, "grp": grp}, device_id_type=MESH)
        asks[k].start()
    own = pltpu.make_async_copy(req_out.at[here], req_s.at[here], table_sem.at[here])
    own.start()
    slots = pltpu.make_async_copy(slot_v, slot_s, slot_sem)
    slots.start()
    tables = {}
    for k in steps:
        asks[k].wait_recv()
        tables[k] = pltpu.make_async_copy(req_in.at[k], req_s.at[k], table_sem.at[k])
        tables[k].start()

    sends = {}
    for k in steps:
        tables[k].wait()
        asker = lax.rem(me + (half - k + ndom), ndom)
        if paired:
            served[k, 0] = basis_ref[within(req_s[k, grp, 0], blk_dev)]
            sends[k] = [pltpu.make_async_remote_copy(
                src_ref=served.at[k, 0], dst_ref=fetched.at[k * CAP + grp],
                send_sem=blk_send.at[k, 0], recv_sem=blk_recv.at[k, 0],
                device_id={"dom": asker, "grp": grp}, device_id_type=MESH)]
        else:
            for level in range(CAP):
                served[k, level] = basis_ref[within(req_s[k, level, 0], blk_dev)]
            sends[k] = [pltpu.make_async_remote_copy(
                src_ref=served.at[k, level], dst_ref=fetched.at[k * CAP + level],
                send_sem=blk_send.at[k, level], recv_sem=blk_recv.at[k, level],
                device_id={"dom": asker, "grp": grp}, device_id_type=MESH) for level in range(CAP)]
        for send in sends[k]:
            send.start()
    own.wait()
    for level in range(CAP):
        mine = basis_ref[within(req_s[here, level, 0], blk_dev)]
        fetched[here * CAP + level] = mine
        turned[here * CAP + level] = mine.T

    forwards = {}
    for k in steps:
        for send in sends[k]:
            send.wait_recv()
        if paired:
            forwards[k] = pltpu.make_async_remote_copy(
                src_ref=fetched.at[k * CAP + grp], dst_ref=fetched.at[k * CAP + grp],
                send_sem=fwd_send.at[k], recv_sem=fwd_recv.at[k],
                device_id={"dom": me, "grp": 1 - grp}, device_id_type=MESH)
            forwards[k].start()
            turned[k * CAP + grp] = fetched[k * CAP + grp].T
        else:
            for level in range(CAP):
                turned[k * CAP + level] = fetched[k * CAP + level].T
    if paired:
        for k in steps:
            pltpu.make_async_remote_copy(
                src_ref=fetched.at[k * CAP + 1 - grp], dst_ref=fetched.at[k * CAP + 1 - grp],
                send_sem=fwd_send.at[k], recv_sem=fwd_recv.at[k],
                device_id={"dom": me, "grp": 1 - grp}, device_id_type=MESH).wait_recv()
            turned[k * CAP + 1 - grp] = fetched[k * CAP + 1 - grp].T
    for k in steps:
        asks[k].wait_send()
        for send in sends[k]:
            send.wait_send()
        if paired:
            forwards[k].wait_send()
    slots.wait()
    for load in loads:
        load.wait()

    count = count_ref[0]
    acc[...] = jnp.zeros_like(acc)

    def project(step, carry):
        rights, lefts = [], []
        for i in range(GROUP):
            t = step * GROUP + i
            right = dot(tiles[t], fetched[within(slot_s[1, t], NEAR * CAP)])
            live = jnp.where(t < count, 1.0, 0.0)
            rights.append((right * live).astype(jnp.bfloat16))
            lefts.append(turned[within(slot_s[0, t], NEAR * CAP)])
        acc[...] += dot(jnp.concatenate(lefts, axis=1), jnp.concatenate(rights, axis=0))
        return carry

    lax.fori_loop(0, ntile // GROUP, project, 0)

    rows = part.shape[1]
    for j in range(ndom):
        part[j] = acc[j * rows:(j + 1) * rows, :]

    scatters = []
    for s in range(1, ndom):
        peer = lax.rem(me + s, ndom)
        scatters.append(pltpu.make_async_remote_copy(
            src_ref=part.at[peer], dst_ref=rs_in.at[s], send_sem=rs_send.at[s], recv_sem=rs_recv.at[s],
            device_id={"dom": peer, "grp": grp}, device_id_type=MESH))
        scatters[-1].start()
    total = part[me]
    for s in range(1, ndom):
        scatters[s - 1].wait_recv()
        total = total + rs_in[s]
    ag[me] = total.astype(jnp.bfloat16)

    gathers = []
    for s in range(1, ndom):
        peer = lax.rem(me + s, ndom)
        gathers.append(pltpu.make_async_remote_copy(
            src_ref=ag.at[me], dst_ref=ag.at[me], send_sem=ag_send.at[s], recv_sem=ag_recv.at[s],
            device_id={"dom": peer, "grp": grp}, device_id_type=MESH))
        gathers[-1].start()
    for s in range(1, ndom):
        source = lax.rem(me + (ndom - s), ndom)
        pltpu.make_async_remote_copy(
            src_ref=ag.at[source], dst_ref=ag.at[source], send_sem=ag_send.at[s], recv_sem=ag_recv.at[s],
            device_id={"dom": source, "grp": grp}, device_id_type=MESH).wait_recv()
    for j in range(ndom):
        out_ref[j * rows:(j + 1) * rows, :] = ag[j].astype(jnp.float32)
    for s in range(1, ndom):
        scatters[s - 1].wait_send()
        gathers[s - 1].wait_send()


def on_device(ndom, ngrp, tangent_tiles, tile_blocks, block_home, tile_count, basis):
    ntile, block, _ = tangent_tiles.shape
    rank = basis.shape[1]
    nblk = block_home.shape[0]
    blk_dev = basis.shape[0] // block
    rows = rank // ndom
    vmem = pl.BlockSpec(memory_space=pltpu.VMEM)
    bf16, f32, i32 = jnp.bfloat16, jnp.float32, jnp.int32
    dma = pltpu.SemaphoreType.DMA
    return pl.pallas_call(
        functools.partial(kernel, ndom, ngrp),
        out_shape=jax.ShapeDtypeStruct((rank, rank), f32),
        in_specs=[vmem, vmem, pl.BlockSpec(memory_space=pltpu.SMEM), vmem, pl.BlockSpec(memory_space=pl.ANY)],
        out_specs=vmem,
        scratch_shapes=[
            pltpu.VMEM((ntile, block, block), bf16),
            pltpu.VMEM((NEAR, CAP, 128), i32),
            pltpu.VMEM((NEAR, CAP, 128), i32),
            pltpu.SMEM((NEAR, CAP, 128), i32),
            pltpu.VMEM((2, ntile), i32),
            pltpu.SMEM((2, ntile), i32),
            pltpu.VMEM((NEAR, CAP, block, rank), bf16),
            pltpu.VMEM((NEAR * CAP, block, rank), bf16),
            pltpu.VMEM((NEAR * CAP, rank, block), bf16),
            pltpu.VMEM((ndom, rows, rank), f32),
            pltpu.VMEM((ndom, rows, rank), f32),
            pltpu.VMEM((ndom, rows, rank), bf16),
            pltpu.VMEM((rank, rank), f32),
            dma((LOADS,)),
            dma((NEAR,)), dma((NEAR,)), dma((NEAR,)), dma,
            dma((NEAR, CAP)), dma((NEAR, CAP)), dma((NEAR,)), dma((NEAR,)),
            dma((ndom,)), dma((ndom,)), dma((ndom,)), dma((ndom,)),
        ],
        compiler_params=pltpu.CompilerParams(collective_id=0, has_side_effects=True),
    )(tile_blocks.T, block_home.reshape(1, nblk), tile_count, basis.reshape(blk_dev, block, rank), tangent_tiles)


def solution(mesh):
    return jax.shard_map(
        functools.partial(on_device, mesh.shape["dom"], mesh.shape["grp"]),
        mesh=mesh,
        in_specs=(P(("grp", "dom"), None, None), P("dom", None), P(), P("dom"), P("dom", None)),
        out_specs=P("grp", None),
        check_vma=False,
    )
```

time: 212 us -> 45.1 us (0.21)
  waiting for transfers between devices: 122 us -> 0 us
  Pallas kernels: 0 us -> 42.6 us
  local copies, waits for them, and re-layouts: 31.4 us -> 1.67 us
  starting transfers between devices: 23.9 us -> 0 us
  matrix products: 18 us -> 0 us
  between operations: 14.5 us -> 0.66 us
    psum x1 -> x0, waiting for transfers between devices: 104 us -> none  [on_device(): reduced = lax.psum(partial_sum, 'dom')]
    pallas_call x0 -> x1, Pallas kernels: none -> 42.6 us  [on_device(): pl.pallas_call(functools.partial(kernel, ndom, ngrp), out_shape=jax.Shape...]
    gather x26 -> x0, local copies, waits for them, and re-layouts: 26 us -> none  [the longest x8 12.8 us: project(): rows = jnp.take(fetched, link_set[:, 0], axis=0)]
    ppermute x14 -> x0, starting transfers between devices: 23.9 us -> none  [shifted(): return lax.ppermute(value, axis, pairs)]
    dot_general x8 -> x0, matrix products: 18 us -> none  [project(): jnp.einsum('ar,as->rs', rows.reshape(GROUP * block, rank), right.reshape(...]
    ppermute x14 -> x0, waiting for transfers between devices: 17.6 us -> none  [shifted(): return lax.ppermute(value, axis, pairs)]
  transfers between devices with their start and end apart: 15 -> 0, of which waited for: 5 -> 0; matrix products, arithmetic and copies ran while one was open for 2% -> 0% of each run, Pallas kernels for 0% -> 0%
where the time goes in v1:
time: 45.1 us; the launch traced here: 44.9 us
  Pallas kernels  42.6 us (94%)
  local copies, waits for them, and re-layouts  1.67 us (4%)
  between operations  0.66 us (1%)
    pallas_call x1, Pallas kernels, on_device(): pl.pallas_call(functools.partial(kernel, ndom, ngrp), out_shape=jax.Shape...  42.6 us
    unnamed x1, local copies, waits for them, and re-layouts  1.67 us

profile of v1, /device:TPU:0, one launch (start us, length us, event | category | flops | bytes accessed | tf_op | source)
XLA Modules:
  0.0 44.9 jit_solution(6016485814460006330)
XLA Ops:
  0.7 42.6 %shard_map.55 = f32[256,256]{1,0:T(8,128)} custom-call(s32[2,128]{1,0:T(2,128)} %bitcast.4, s32[1,128]{1,0:T(1,128)} %bitcast.5, s32[1]{0:T(128)S(6)} %copy.7.count_ref, bf16[8,128,256]{2,1,0:T(8,128)(2,1)} %bitcast.3, bf16[128,128,128]{2,1,0:T(8,128)(2,1)} %tiles_hbm.1), custom_call_target="tpu_custom_call" | custom-call | tf_op jit(solution)/shard_map/pallas_call | solution.py:218
  43.2 1.7 %copy.8 = f32[256,256]{1,0:T(8,128)} copy(f32[256,256]{1,0:T(8,128)} %shard_map.55) | data formatting | bytes 524288

commit v2 on v1

--- a/solution.py
+++ b/solution.py
@@ -9,7 +9,7 @@
 
 CAP = 2
 NEAR = 8
-GROUP = 16
+GROUP = 32
 LOADS = 4
 MESH = pl.DeviceIdType.MESH
 
@@ -22,8 +22,8 @@
     return jnp.minimum(jnp.maximum(index, 0), size - 1)
 
 
-def kernel(ndom, ngrp, tb_ref, home_ref, count_ref, basis_ref, tiles_hbm, out_ref,
-           tiles, req_out, req_in, req_s, slot_v, slot_s, served, fetched, turned,
+def kernel(ndom, ngrp, tb_hbm, home_hbm, count_hbm, basis_hbm, tiles_hbm, out_hbm,
+           tb_ref, home_ref, count_ref, basis_ref, in_sem, out_sem, tiles, req_out, req_in, req_s, slot_v, slot_s, served, fetched, turned,
            part, rs_in, ag, acc, tile_sem, req_send, req_recv, table_sem, slot_sem,
            blk_send, blk_recv, fwd_send, fwd_recv, rs_send, rs_recv, ag_send, ag_recv):
     me = lax.axis_index("dom")
@@ -42,6 +42,14 @@
     if paired:
         pl.semaphore_signal(barrier, inc=1, device_id={"dom": me, "grp": 1 - grp}, device_id_type=MESH)
 
+    inputs = [
+        pltpu.make_async_copy(tb_hbm, tb_ref, in_sem.at[0]),
+        pltpu.make_async_copy(home_hbm, home_ref, in_sem.at[1]),
+        pltpu.make_async_copy(count_hbm, count_ref, in_sem.at[2]),
+        pltpu.make_async_copy(basis_hbm, basis_ref, in_sem.at[3]),
+    ]
+    for load in inputs:
+        load.start()
     per = ntile // LOADS
     loads = [
         pltpu.make_async_copy(tiles_hbm.at[pl.ds(i * per, per)], tiles.at[pl.ds(i * per, per)], tile_sem.at[i])
@@ -50,6 +58,8 @@
     for load in loads:
         load.start()
 
+    for load in inputs[:3]:
+        load.wait()
     pos = lax.broadcasted_iota(jnp.int32, (nblk, nblk), 0)
     other = lax.broadcasted_iota(jnp.int32, (nblk, nblk), 1)
     moved = jnp.where(pos == home_ref[...], 1.0, 0.0).astype(jnp.bfloat16)
@@ -75,12 +85,15 @@
     window = jnp.minimum(window, NEAR - 1)
     slot_map = (window * CAP).astype(jnp.float32) + order
     slot_map = jnp.broadcast_to(slot_map[:, 0:1], (nblk, ntile))
-    slot_v[0:1, :] = jnp.sum(at_row * slot_map, axis=0, keepdims=True).astype(jnp.int32)
+    row_slot = jnp.sum(at_row * slot_map, axis=0, keepdims=True).astype(jnp.int32)
+    live = lax.broadcasted_iota(jnp.int32, (1, ntile), 1) < count_ref[0]
+    slot_v[0:1, :] = jnp.where(live, row_slot, NEAR * CAP)
+    turned[NEAR * CAP] = jnp.zeros(turned.shape[1:], turned.dtype)
     slot_v[1:2, :] = jnp.sum(at_col * slot_map, axis=0, keepdims=True).astype(jnp.int32)
 
     pl.semaphore_wait(barrier, ndom - 1 + (1 if paired else 0))
 
-    steps = [k for k in range(NEAR) if k != here]
+    steps = sorted((k for k in range(NEAR) if k != here), key=lambda k: -abs(k - here))
     asks = {}
     for k in steps:
         target = lax.rem(me + (k - half + ndom), ndom)
@@ -98,6 +111,7 @@
         tables[k] = pltpu.make_async_copy(req_in.at[k], req_s.at[k], table_sem.at[k])
         tables[k].start()
 
+    inputs[3].wait()
     sends = {}
     for k in steps:
         tables[k].wait()
@@ -154,7 +168,6 @@
     for load in loads:
         load.wait()
 
-    count = count_ref[0]
     acc[...] = jnp.zeros_like(acc)
 
     def project(step, carry):
@@ -162,9 +175,8 @@
         for i in range(GROUP):
             t = step * GROUP + i
             right = dot(tiles[t], fetched[within(slot_s[1, t], NEAR * CAP)])
-            live = jnp.where(t < count, 1.0, 0.0)
-            rights.append((right * live).astype(jnp.bfloat16))
-            lefts.append(turned[within(slot_s[0, t], NEAR * CAP)])
+            rights.append(right.astype(jnp.bfloat16))
+            lefts.append(turned[within(slot_s[0, t], NEAR * CAP + 1)])
         acc[...] += dot(jnp.concatenate(lefts, axis=1), jnp.concatenate(rights, axis=0))
         return carry
 
@@ -199,11 +211,12 @@
         pltpu.make_async_remote_copy(
             src_ref=ag.at[source], dst_ref=ag.at[source], send_sem=ag_send.at[s], recv_sem=ag_recv.at[s],
             device_id={"dom": source, "grp": grp}, device_id_type=MESH).wait_recv()
-    for j in range(ndom):
-        out_ref[j * rows:(j + 1) * rows, :] = ag[j].astype(jnp.float32)
+    result = pltpu.make_async_copy(ag, out_hbm, out_sem)
+    result.start()
     for s in range(1, ndom):
         scatters[s - 1].wait_send()
         gathers[s - 1].wait_send()
+    result.wait()
 
 
 def on_device(ndom, ngrp, tangent_tiles, tile_blocks, block_home, tile_count, basis):
@@ -212,15 +225,20 @@
     nblk = block_home.shape[0]
     blk_dev = basis.shape[0] // block
     rows = rank // ndom
-    vmem = pl.BlockSpec(memory_space=pltpu.VMEM)
+    whole = pl.BlockSpec(memory_space=pl.ANY)
     bf16, f32, i32 = jnp.bfloat16, jnp.float32, jnp.int32
     dma = pltpu.SemaphoreType.DMA
-    return pl.pallas_call(
+    reduced = pl.pallas_call(
         functools.partial(kernel, ndom, ngrp),
-        out_shape=jax.ShapeDtypeStruct((rank, rank), f32),
-        in_specs=[vmem, vmem, pl.BlockSpec(memory_space=pltpu.SMEM), vmem, pl.BlockSpec(memory_space=pl.ANY)],
-        out_specs=vmem,
+        out_shape=jax.ShapeDtypeStruct((ndom, rows, rank), bf16),
+        in_specs=[whole] * 5,
+        out_specs=whole,
         scratch_shapes=[
+            pltpu.VMEM((2, ntile), i32),
+            pltpu.VMEM((1, nblk), i32),
+            pltpu.SMEM((1,), i32),
+            pltpu.VMEM((blk_dev, block, rank), bf16),
+            dma((4,)), dma,
             pltpu.VMEM((ntile, block, block), bf16),
             pltpu.VMEM((NEAR, CAP, 128), i32),
             pltpu.VMEM((NEAR, CAP, 128), i32),
@@ -229,7 +247,7 @@
             pltpu.SMEM((2, ntile), i32),
             pltpu.VMEM((NEAR, CAP, block, rank), bf16),
             pltpu.VMEM((NEAR * CAP, block, rank), bf16),
-            pltpu.VMEM((NEAR * CAP, rank, block), bf16),
+            pltpu.VMEM((NEAR * CAP + 1, rank, block), bf16),
             pltpu.VMEM((ndom, rows, rank), f32),
             pltpu.VMEM((ndom, rows, rank), f32),
             pltpu.VMEM((ndom, rows, rank), bf16),
@@ -240,7 +258,9 @@
             dma((ndom,)), dma((ndom,)), dma((ndom,)), dma((ndom,)),
         ],
         compiler_params=pltpu.CompilerParams(collective_id=0, has_side_effects=True),
-    )(tile_blocks.T, block_home.reshape(1, nblk), tile_count, basis.reshape(blk_dev, block, rank), tangent_tiles)
+    )(tile_blocks.T, block_home.reshape(1, nblk), tile_count,
+      basis.reshape(blk_dev, block, rank), tangent_tiles)
+    return reduced.reshape(rank, rank).astype(f32)
 
 
 def solution(mesh):

time: 45.1 us -> 42.8 us (0.949)
  Pallas kernels: 42.6 us -> 40.4 us
  local copies, waits for them, and re-layouts: 1.67 us -> 0 us
  other arithmetic: 0 us -> 1.63 us
    pallas_call x1, Pallas kernels: 42.6 us -> 40.4 us  [on_device(): pl.pallas_call(functools.partial(kernel, ndom, ngrp), out_shape=jax.Shape...]
    unnamed x1 -> x0, local copies, waits for them, and re-layouts: 1.67 us -> none
    convert_element_type x0 -> x1, other arithmetic: none -> 1.63 us  [on_device(): return reduced.reshape(rank, rank).astype(f32)]
where the time goes in v2:
time: 42.8 us; the launch traced here: 42.7 us
  Pallas kernels  40.4 us (94%)
  other arithmetic  1.63 us (4%)
  between operations  0.66 us (2%)
    pallas_call x1, Pallas kernels, on_device(): pl.pallas_call(functools.partial(kernel, ndom, ngrp), out_shape=jax.Shape...  40.4 us
    convert_element_type x1, other arithmetic, on_device(): return reduced.reshape(rank, rank).astype(f32)  1.63 us

profile of v2, /device:TPU:0, one launch (start us, length us, event | category | flops | bytes accessed | tf_op | source)
XLA Modules:
  0.0 42.7 jit_solution(16872953279627812133)
XLA Ops:
  0.7 40.4 %shard_map.55 = bf16[16,16,256]{2,1,0:T(8,128)(2,1)} custom-call(s32[2,128]{1,0:T(2,128)} %bitcast.7, s32[1,128]{1,0:T(1,128)} %bitcast.8, s32[1]{0:T(128)S(6)} %copy.6.count_hbm, bf16[8,128,256]{2,1,0:T(8,128)(2,1)} %bitcast.6, bf16[128,128,128]{2,1,0:T(8,128)(2,1)} %tiles_hbm.1), custom_call_target="tpu_custom_call" | custom-call | tf_op jit(solution)/shard_map/pallas_call | solution.py:231
  41.0 1.6 %bitcast_convert_fusion = f32[256,256]{1,0:T(8,128)} fusion(bf16[16,16,256]{2,1,0:T(8,128)(2,1)} %shard_map.55), kind=kLoop, calls=%fused_computation | loop fusion | flops 65536 | bytes 393216 | tf_op jit(solution)/shard_map/convert_element_type | solution.py:263
